TPU v7x, 32 devices: a whole 2x2x4 slice. The times are simulated.
32 devices in a mesh: gy: 16 (over z, y, core), gz: 2 (over x).
Axes of the slice: x: 2, y: 2, z: 4, core: 2. Of those that a mesh axis runs over, the one named last changes fastest.
Arguments:
- omega: float32 [3, 256, 128, 128], P(None, 'gy', 'gz'), may hold values from -6 to 6
- velocity: float32 [3, 256, 128, 128], P(None, 'gy', 'gz'), may hold values from -6 to 6
- point_owner: int32 [1152], replicated, may hold values from 0 to 22, as said below
- point_cells: int32 [3, 1152], replicated, may hold values from 1 to 125, as said below
- point_frac: float32 [3, 1152], replicated, may hold values from 0 to 1
- chord: float32 [1152], replicated, may hold values from 0.2 to 1
- twist: float32 [1152], replicated, may hold values from -0.3 to 0.3
- angle_step: int32 [1], replicated, may hold values from 0 to 719
Outputs:
- omega_out: float32 [3, 256, 128, 128], P(None, 'gy', 'gz')
- blade_sources: float32 [3, 1152], replicated
Inputs may be any that keep to these rules, and one draw needn't show every extreme that they name: `point_owner`: turbine t's points lie in spanwise blocks t * 2 to (t + 1) * 2 - 1 and in the 1 vertical blocks from (1) // 2 on; no block holds more than 192 points, and in every turbine one block holds exactly 192. `point_cells`: streamwise cells lie in 1 to 125, spanwise in 1 to 13, vertical in 1 to 61; all points of a turbine share one streamwise cell.
All inputs are finite; a program needn't handle non-finite values.
Results may differ from a plain program's by a relative error of at most 0.0003.
Values sent between devices are 32-bit elements; how exact they have to be, the bound alone decides.
A program may use at most 128 MiB of HBM per device.

v0:
```python
import jax
import jax.numpy as jnp
from jax import lax
from jax.sharding import PartitionSpec as P

TURBINES = 6
BLADES = 3
BP = 64
section_step = 0.4
viscosity = 0.05
tip_speed = 3.0
turn_step = 2.0 * 3.141592653589793 / 720.0


def with_halo(x, sides, width):
    for axis, dim in sides:
        size, length = (lax.axis_size(axis), x.shape[dim])
        up = [(i, (i + 1) % size) for i in range(size - 1)]
        down = [(j, i) for i, j in up]
        last = lax.slice_in_dim(x, length - width, length, axis=dim)
        initial = lax.slice_in_dim(x, 0, width, axis=dim)
        before = lax.ppermute(last, axis, up)
        after = lax.ppermute(initial, axis, down)
        x = jnp.concatenate([before, x, after], axis=dim)
    return x


def remesh_kernel(shift):
    mag = jnp.abs(shift)
    inner = 1.0 - 2.5 * mag * mag + 1.5 * mag * mag * mag
    outer = 0.5 * (2.0 - mag) * (2.0 - mag) * (1.0 - mag)
    return jnp.where(mag < 1.0, inner, jnp.where(mag < 2.0, outer, 0.0))


def shifted(padded, axis, offset):
    index = []
    for dim in range(4):
        if dim == 0:
            index.append(slice(None))
        elif dim == axis:
            index.append(slice(offset, offset + padded.shape[dim] - 4))
        else:
            index.append(slice(2, padded.shape[dim] - 2))
    return padded[tuple(index)]


def centered_first(padded, axis):
    return (
        shifted(padded, axis, 0)
        - 8.0 * shifted(padded, axis, 1)
        + 8.0 * shifted(padded, axis, 3)
        - shifted(padded, axis, 4)
    ) / 12.0


def centered_second(padded, axis):
    return (
        -shifted(padded, axis, 0)
        + 16.0 * shifted(padded, axis, 1)
        - 30.0 * shifted(padded, axis, 2)
        + 16.0 * shifted(padded, axis, 3)
        - shifted(padded, axis, 4)
    ) / 12.0


def remesh_padded(field, displace, axis):
    length = field.shape[axis] - 4
    total = jnp.zeros(field.shape[:axis] + (length,) + field.shape[axis + 1 :], jnp.float32)
    for offset in range(-2, 3):
        start = 2 - offset
        part = lax.slice_in_dim(field, start, start + length, axis=axis)
        moved = lax.slice_in_dim(displace, start, start + length, axis=axis - 1)
        total = total + remesh_kernel(offset - moved)[None] * part
    return total


def blade_forces(point_velocity, chord, twist, angle_step):
    count = point_velocity.shape[1]
    points = jnp.arange(count, dtype=jnp.int32)
    station = points % BP
    blade = points // BP % BLADES
    theta = angle_step[0].astype(
        jnp.float32
    ) * turn_step + 2.0 * 3.141592653589793 / 3.0 * blade.astype(jnp.float32)
    radius = (station.astype(jnp.float32) + 0.5) / BP
    cos_t = jnp.cos(theta)
    sin_t = jnp.sin(theta)
    rel_x = point_velocity[0]
    rel_y = point_velocity[1] + tip_speed * radius * sin_t
    rel_z = point_velocity[2] - tip_speed * radius * cos_t
    rel_t = -sin_t * rel_y + cos_t * rel_z
    speed = jnp.sqrt(rel_x * rel_x + rel_t * rel_t + 1.0)
    gamma = 3.141592653589793 * chord * (rel_x * jnp.cos(twist) + rel_t * jnp.sin(twist))
    blades = gamma.reshape(-1, BP)
    before = jnp.concatenate([jnp.zeros((blades.shape[0], 1), jnp.float32), blades[:, :-1]], axis=1)
    shed = (blades - before).reshape(-1)
    return jnp.stack(
        [
            shed * rel_x / speed,
            gamma * cos_t + shed * rel_y / speed,
            gamma * sin_t + shed * rel_z / speed,
        ]
    )


def point_tables(
    cells,
    fracs,
    owner_span,
    owner_vert,
    span_index,
    vert_index,
    span_cells,
    vert_cells,
    axial_cells,
):
    rows_x = jnp.arange(axial_cells, dtype=jnp.int32)
    rows_y = jnp.arange(span_cells, dtype=jnp.int32)
    rows_z = jnp.arange(vert_cells, dtype=jnp.int32)
    gap_x = rows_x[:, None] - cells[0][None, :]
    gap_y = (
        span_index * span_cells
        + rows_y[:, None]
        - owner_span[None, :] * span_cells
        - cells[1][None, :]
    )
    gap_z = (
        vert_index * vert_cells
        + rows_z[:, None]
        - owner_vert[None, :] * vert_cells
        - cells[2][None, :]
    )
    table_x = remesh_kernel(gap_x.astype(jnp.float32) - fracs[0][None, :])
    table_y = remesh_kernel(gap_y.astype(jnp.float32) - fracs[1][None, :])
    table_z = remesh_kernel(gap_z.astype(jnp.float32) - fracs[2][None, :])
    return (table_x, table_y, table_z)


def on_device(omega, velocity, point_owner, point_cells, point_frac, chord, twist, angle_step):
    span_cells, vert_cells, axial_cells = (omega.shape[1], omega.shape[2], omega.shape[3])
    span_count = lax.axis_size("gy")
    vert_count = lax.axis_size("gz")
    span_index = lax.axis_index("gy")
    vert_index = lax.axis_index("gz")
    owner_span = point_owner // vert_count
    owner_vert = point_owner % vert_count
    highest = lax.Precision.HIGHEST
    busiest = 2 * (BLADES * BP) // (span_count // TURBINES * max(vert_count // 2, 1))
    my_block = span_index * vert_count + vert_index
    points = jnp.arange(point_owner.shape[0], dtype=jnp.int32)
    ranking = jnp.where(point_owner == my_block, points, points + point_owner.shape[0])
    picked = jnp.argsort(ranking, stable=True)[:busiest]
    selector = (picked[:, None] == points[None, :]).astype(jnp.float32)
    table_x, table_y, table_z = point_tables(
        point_cells[:, picked],
        point_frac[:, picked],
        owner_span[picked],
        owner_vert[picked],
        span_index,
        vert_index,
        span_cells,
        vert_cells,
        axial_cells,
    )
    columns = jnp.dot(
        velocity.reshape(-1, axial_cells),
        table_x,
        precision=highest,
        preferred_element_type=jnp.float32,
    )
    columns = columns.reshape(3, span_cells, vert_cells, -1)
    compact = jnp.einsum("cyzq,yq,zq->cq", columns, table_y, table_z, precision=highest)
    partial_velocity = jnp.dot(
        compact, selector, precision=highest, preferred_element_type=jnp.float32
    )
    point_velocity = lax.psum(partial_velocity, ("gy", "gz"))
    sources = blade_forces(point_velocity, chord, twist, angle_step)
    local_sources = sources[:, picked]
    spread = jnp.einsum("cq,yq,zq->cyzq", local_sources, table_y, table_z, precision=highest)
    smear = jnp.dot(
        spread.reshape(-1, spread.shape[3]),
        table_x.T,
        precision=highest,
        preferred_element_type=jnp.float32,
    )
    smear = smear.reshape(3, span_cells, vert_cells, axial_cells)
    omega_rim, velocity_rim = (
        with_halo(omega, (("gy", 1), ("gz", 2)), 2),
        with_halo(velocity, (("gy", 1), ("gz", 2)), 2),
    )
    axial_pads = ((0, 0), (0, 0), (0, 0), (2, 2))
    omega_pad = jnp.pad(omega_rim, axial_pads)
    velocity_pad = jnp.pad(velocity_rim, axial_pads)
    stretch = jnp.zeros_like(omega)
    laplace = jnp.zeros_like(omega)
    for axis in range(3):
        stretch = stretch + omega[2 - axis][None] * centered_first(velocity_pad, 3 - axis)
        laplace = laplace + centered_second(omega_pad, axis + 1)
    section = omega + section_step * (stretch + viscosity * laplace + smear)
    shift_x = jnp.clip(section_step * velocity[0], -1.0, 1.0)
    moved_x = remesh_padded(
        jnp.pad(section, axial_pads), jnp.pad(shift_x, ((0, 0), (0, 0), (2, 2))), 3
    )
    shift_z = jnp.clip(section_step * velocity_rim[2][2 : span_cells + 2, :, :], -1.0, 1.0)
    span_rim = with_halo(moved_x, (("gy", 1),), 2)
    shift_y = jnp.clip(section_step * velocity_rim[1][:, 2 : vert_cells + 2, :], -1.0, 1.0)
    moved_mid = remesh_padded(span_rim, shift_y, 1)
    moved_y = with_halo(moved_mid, (("gz", 2),), 2)
    omega_out = remesh_padded(moved_y, shift_z, 2)
    return (omega_out, sources)


def solution(mesh):
    in_specs = (P(None, "gy", "gz", None), P(None, "gy", "gz", None), P(), P(), P(), P(), P(), P())
    out_specs = (P(None, "gy", "gz", None), P())
    return jax.shard_map(
        on_device, mesh=mesh, in_specs=in_specs, out_specs=out_specs, check_vma=False
    )
```

profile of v0, /device:TPU:10, one launch (start us, length us, event | category | flops | bytes accessed | tf_op | source)
XLA Modules:
  0.0 163.6 jit_solution(6236119518289551892)
XLA Ops:
  0.6 1.8 %fusion.252 = (f32[3,2,64,128]{3,2,1,0:T(8,128)}, f32[3,2,64,128]{3,2,1,0:T(8,128)}) fusion(f32[3,16,64,128]{3,2,1,0:T(8,128)} %param.9), kind=kLoop, calls=%fused_computation.439 | loop fusion | bytes 786432 | tf_op jit(solution)/shard_map/slice | solution.py:21
  2.5 2.0 %collective-permute-start = (f32[3,2,64,128]{3,2,1,0:T(8,128)}, f32[3,2,64,128]{3,2,1,0:T(8,128)}, u32[]{:S(2)}, u32[]{:S(2)}) collective-permute-start(f32[3,2,64,128]{3,2,1,0:T(8,128)} %get-tuple-element.33), channel_id=1, source_target_pairs={{0,2},{2,4},{4,6},{6,8},{8,10},{10,12},{12,14},{14,16},{16,18},{18... | collective-permute-start | bytes 589832 | tf_op jit(solution)/shard_map/ppermute | solution.py:22
  4.5 4.5 %collective-permute-start.1 = (f32[3,2,64,128]{3,2,1,0:T(8,128)}, f32[3,2,64,128]{3,2,1,0:T(8,128)}, u32[]{:S(2)}, u32[]{:S(2)}) collective-permute-start(f32[3,2,64,128]{3,2,1,0:T(8,128)} %get-tuple-element.32), channel_id=1, source_target_pairs={{2,0},{4,2},{6,4},{8,6},{10,8},{12,10},{14,12},{16,14},{18,16},{20... | collective-permute-start | bytes 589832 | tf_op jit(solution)/shard_map/ppermute | solution.py:23
  9.1 1.7 %fusion.253 = (f32[3,2,64,128]{3,2,1,0:T(8,128)S(1)}, f32[3,2,64,128]{3,2,1,0:T(8,128)}) fusion(f32[3,16,64,128]{3,2,1,0:T(8,128)} %param.8), kind=kLoop, calls=%fused_computation.440 | loop fusion | bytes 786432 | tf_op jit(solution)/shard_map/slice | solution.py:21
  10.8 2.0 %collective-permute-start.4 = (f32[3,2,64,128]{3,2,1,0:T(8,128)}, f32[3,2,64,128]{3,2,1,0:T(8,128)}, u32[]{:S(2)}, u32[]{:S(2)}) collective-permute-start(f32[3,2,64,128]{3,2,1,0:T(8,128)} %get-tuple-element.35), channel_id=1, source_target_pairs={{0,2},{2,4},{4,6},{6,8},{8,10},{10,12},{12,14},{14,16},{16,18},{18... | collective-permute-start | bytes 589832 | tf_op jit(solution)/shard_map/ppermute | solution.py:22
  12.8 4.5 %collective-permute-start.5 = (f32[3,2,64,128]{3,2,1,0:T(8,128)S(1)}, f32[3,2,64,128]{3,2,1,0:T(8,128)}, u32[]{:S(2)}, u32[]{:S(2)}) collective-permute-start(f32[3,2,64,128]{3,2,1,0:T(8,128)S(1)} %get-tuple-element.34), channel_id=1, source_target_pairs={{2,0},{4,2},{6,4},{8,6},{10,8},{12,10},{14,12},{16,14},{18,16},{20... | collective-permute-start | bytes 589832 | tf_op jit(solution)/shard_map/ppermute | solution.py:23
  17.4 5.0 %sort.17 = (s32[1152]{0:T(1024)}, s32[1152]{0:T(1024)S(1)}) sort(s32[1152]{0:T(1024)S(1)} %get-tuple-element.63, s32[1152]{0:T(1024)S(1)} %iota.43), dimensions={0}, to_apply=%region_0.1 | sort | flops 12672 | bytes 18432 | tf_op jit(solution)/shard_map/jit(argsort)/sort | solution.py:152
  22.5 1.4 gather_fusion.3
  24.0 0.2 copy.14
  24.2 0.7 gather_fusion.1
  24.9 0.3 slice_reduce_fusion.5
  25.2 0.2 copy.15
  25.5 0.7 gather_fusion.2
  26.2 0.3 slice_reduce_fusion.4
  26.5 0.5 copy-done.19
  27.0 3.6 %convolution_bitcast_fusion = f32[3072,192]{0,1:T(8,128)} fusion(f32[3072,128]{1,0:T(8,128)S(1)} %bitcast.49, f32[192]{0:T(256)S(1)} %get-tuple-element.8, s32[192]{0:T(256)S(1)} %get-tuple-element.5), kind=kOutput, calls=%fused_computation.18 | convolution fusion | flops 906461184 | bytes 3933696 | tf_op jit(solution)/shard_map/dot_general | solution.py:165
  30.6 2.2 %copy.29 = f32[3072,192]{1,0:T(8,128)S(1)} copy(f32[3072,192]{0,1:T(8,128)} %convolution_bitcast_fusion) | data formatting | bytes 4718592
  32.8 0.1 fusion.188
  33.0 0.4 multiply_reduce_fusion
  33.4 0.2 copy.25
  33.7 1.4 gather_fusion
  35.1 0.1 fusion.223
  35.2 0.1 copy.26
  35.3 1.4 fusion.255
  36.7 0.5 fusion.77
  37.2 40.4 %psum.7 = f32[3,1152]{1,0:T(4,128)S(1)} all-reduce(f32[3,1152]{1,0:T(4,128)S(1)} %fusion.77), channel_id=1, replica_groups=mesh['gy'=16,'gz'=2] {'gy','gz'}, use_global_device_ids=true, to_apply=%region_1.2 | all-reduce | flops 3456 | bytes 27648 | tf_op jit(solution)/shard_map/psum | solution.py:176
  78.3 0.1 add_multiply_fusion
  78.5 0.1 reshape.179
  78.7 1.2 multiply_bitcast_fusion.2
  79.9 0.8 copy-done.1
  80.7 1.3 fusion.104
  82.0 0.2 rsqrt_multiply_fusion
  82.2 0.1 divide_add_fusion.1
  82.4 1.1 copy.17
  83.4 1.7 %gather_fusion.4 = f32[192,3]{1,0:T(8,128)S(1)} fusion(f32[3,1152]{0,1:T(8,128)} %copy.17, s32[1024]{0:T(1024)S(1)} %pad_clamp_fusion), kind=kCustom, calls=%fused_computation.4 | custom fusion | bytes 5376 | tf_op jit(solution)/shard_map/gather | solution.py:178
  85.3 4.3 %fusion.93 = (f32[16,64,128]{2,1,0:T(8,128)}, f32[16,64,128]{2,1,0:T(8,128)}, f32[16,64,128]{2,1,0:T(8,128)}, f32[16,64,128]{2,1,0:T(8,128)}) fusion(f32[16,64,128]{2,1,0:T(8,128)} %get-tuple-element.22), kind=kLoop, calls=%fused_computation.199 | loop fusion | flops 9437184 | bytes 2621440 | tf_op jit(solution)/shard_map/jit(_where)/select_n | solution.py:32
  89.6 0.6 broadcast_multiply_fusion
  90.2 1.0 constant_dynamic-update-slice_fusion.4
  91.2 0.6 constant_dynamic-update-slice_fusion.3
  91.8 1.2 constant_dynamic-update-slice_fusion.5
  93.1 1.3 collective-permute-start.2
  94.4 4.7 %collective-permute-start.3 = (f32[3,20,2,128]{3,2,1,0:T(2,128)S(1)}, f32[3,20,2,128]{3,2,1,0:T(2,128)S(1)}, u32[]{:S(2)}, u32[]{:S(2)}) collective-permute-start(f32[3,20,2,128]{3,2,1,0:T(2,128)S(1)} %get-tuple-element.14), channel_id=1, source_target_pairs={{1,0},{3,2},{5,4},{7,6},{9,8},{11,10},{13,12},{15,14},{17,16},{19,... | collective-permute-start | bytes 184328 | tf_op jit(solution)/shard_map/ppermute | solution.py:23
  99.1 1.0 constant_dynamic-update-slice_fusion.8
  100.1 0.6 constant_dynamic-update-slice_fusion.7
  100.7 1.2 constant_dynamic-update-slice_fusion.9
  102.0 1.3 collective-permute-start.6
  103.3 4.5 %collective-permute-start.7 = (f32[3,20,2,128]{3,2,1,0:T(2,128)S(1)}, f32[3,20,2,128]{3,2,1,0:T(2,128)S(1)}, u32[]{:S(2)}, u32[]{:S(2)}) collective-permute-start(f32[3,20,2,128]{3,2,1,0:T(2,128)S(1)} %get-tuple-element.16), channel_id=1, source_target_pairs={{1,0},{3,2},{5,4},{7,6},{9,8},{11,10},{13,12},{15,14},{17,16},{19,... | collective-permute-start | bytes 184328 | tf_op jit(solution)/shard_map/ppermute | solution.py:23
  107.9 1.7 %pad_maximum_fusion = f32[3,20,68,128]{3,2,1,0:T(8,128)} fusion(f32[3,20,2,128]{3,2,1,0:T(2,128)S(1)} %collective-permute-done.3, f32[3,20,64,128]{3,2,1,0:T(8,128)S(1)} %get-tuple-element.53, f32[3,20,2,128]{3,2,1,0:T(2,128)S(1)} %collective-permute-done.2), kind=kLoop, calls=%fused_computation.23 | loop fusion | flops 1044480 | bytes 4177920 | tf_op jit(solution)/shard_map/concatenate | solution.py:24
  109.6 1.2 slice_bitcast_fusion
  110.8 3.5 %select_maximum_fusion = f32[3,20,68,132]{3,2,1,0:T(8,128)} fusion(f32[3,20,2,128]{3,2,1,0:T(2,128)S(1)} %collective-permute-done.7, f32[3,20,64,128]{3,2,1,0:T(8,128)S(1)} %get-tuple-element.57, f32[3,20,2,128]{3,2,1,0:T(2,128)S(1)} %collective-permute-done.6), kind=kLoop, calls=%fused_computation.15 | loop fusion | flops 4308480 | bytes 4243200 | tf_op jit(solution)/shard_map/concatenate | solution.py:24
  114.4 20.4 %fusion.30 = f32[3,16,64,128]{3,2,1,0:T(8,128)} fusion(f32[3,16,64,128]{3,2,1,0:T(8,128)S(1)} %copy-done.2, f32[3,20,64,128]{3,2,1,0:T(8,128)} %copy-done.4, f32[3,20,2,128]{3,2,1,0:T(2,128)S(1)} %collective-permute-done.7, f32[3,20,2,128]{3,2,1,0:T(2,128)S(1)} %collective-permute-done.6, f32[3,20,64,128]{3,2,1,0:T(8,128)} %copy-done.3, ...), kind=kOutput, calls=%fused_computation.70 | convolution fusion | flops 929464320 | bytes 29947392 | tf_op jit(solution)/shard_map/dot_general | solution.py:180
  134.7 6.4 %fusion.48 = f32[3,16,64,128]{3,2,1,0:T(8,128)S(1)} fusion(f32[3,16,64,128]{3,2,1,0:T(8,128)} %fusion.30, f32[16,64,128]{2,1,0:T(8,128)} %get-tuple-element.49, f32[16,64,128]{2,1,0:T(8,128)} %get-tuple-element.48, f32[16,64,128]{2,1,0:T(8,128)S(1)} %copy-done.5, f32[16,64,128]{2,1,0:T(8,128)} %get-tuple-element.47, f32[16,64,128]{2,1,0:T(8,128)} %get-tuple-element.46), kind=kLoop, calls=%fused_computation.88 | loop fusion | flops 3538944 | bytes 5767168 | tf_op jit(solution)/shard_map/add | solution.py:73
  141.2 1.9 %collective-permute-start.8 = (f32[3,2,64,128]{3,2,1,0:T(8,128)S(1)}, f32[3,2,64,128]{3,2,1,0:T(8,128)S(1)}, u32[]{:S(2)}, u32[]{:S(2)}) collective-permute-start(f32[3,2,64,128]{3,2,1,0:T(8,128)S(1)} %get-tuple-element.19), channel_id=1, source_target_pairs={{2,0},{4,2},{6,4},{8,6},{10,8},{12,10},{14,12},{16,14},{18,16},{20... | collective-permute-start | bytes 589832 | tf_op jit(solution)/shard_map/ppermute | solution.py:23
  143.1 2.4 %collective-permute-start.9 = (f32[3,2,64,128]{3,2,1,0:T(8,128)S(1)}, f32[3,2,64,128]{3,2,1,0:T(8,128)S(1)}, u32[]{:S(2)}, u32[]{:S(2)}) collective-permute-start(f32[3,2,64,128]{3,2,1,0:T(8,128)S(1)} %get-tuple-element.20), channel_id=1, source_target_pairs={{0,2},{2,4},{4,6},{6,8},{8,10},{10,12},{12,14},{14,16},{16,18},{18... | collective-permute-start | bytes 589832 | tf_op jit(solution)/shard_map/ppermute | solution.py:22
  145.5 0.1 fusion.78
  145.6 1.5 fusion.88
  147.2 1.1 fusion.80
  148.3 2.7 %collective-permute-done.9 = f32[3,2,64,128]{3,2,1,0:T(8,128)S(1)} collective-permute-done((f32[3,2,64,128]{3,2,1,0:T(8,128)S(1)}, f32[3,2,64,128]{3,2,1,0:T(8,128)S(1)}, u32[]{:S(2)}, u32[]{:S(2)}) %collective-permute-start.9) | collective-permute-done | bytes 196640 | tf_op jit(solution)/shard_map/ppermute | solution.py:22
  151.0 1.3 fusion.15
  152.4 3.1 %collective-permute-start.10 = (f32[3,16,2,128]{3,2,1,0:T(2,128)S(1)}, f32[3,16,2,128]{3,2,1,0:T(2,128)S(1)}, u32[]{:S(2)}, u32[]{:S(2)}) collective-permute-start(f32[3,16,2,128]{3,2,1,0:T(2,128)S(1)} %get-tuple-element.17), channel_id=1, source_target_pairs={{1,0},{3,2},{5,4},{7,6},{9,8},{11,10},{13,12},{15,14},{17,16},{19,... | collective-permute-start | bytes 147464 | tf_op jit(solution)/shard_map/ppermute | solution.py:23
  155.5 1.3 collective-permute-start.11
  156.8 1.7 %fusion.83 = (f32[16,64,128]{2,1,0:T(8,128)S(1)}, f32[16,64,128]{2,1,0:T(8,128)S(1)}, f32[16,64,128]{2,1,0:T(8,128)S(1)}, f32[16,64,128]{2,1,0:T(8,128)S(1)}, f32[16,64,128]{2,1,0:T(8,128)S(1)}) fusion(f32[16,68,128]{2,1,0:T(8,128)S(1)} %fusion.80), kind=kLoop, calls=%fused_computation.189 | loop fusion | flops 11796480 | bytes 5242880 | tf_op jit(solution)/shard_map/jit(_where)/select_n | solution.py:32
  158.5 3.0 %collective-permute-done.11 = f32[3,16,2,128]{3,2,1,0:T(2,128)S(1)} collective-permute-done((f32[3,16,2,128]{3,2,1,0:T(2,128)S(1)}, f32[3,16,2,128]{3,2,1,0:T(2,128)S(1)}, u32[]{:S(2)}, u32[]{:S(2)}) %collective-permute-start.11) | collective-permute-done | bytes 49184 | tf_op jit(solution)/shard_map/ppermute | solution.py:22
  161.5 2.1 %fusion.7 = f32[3,16,64,128]{3,2,1,0:T(8,128)} fusion(f32[3,16,2,128]{3,2,1,0:T(2,128)S(1)} %collective-permute-done.11, f32[3,16,64,128]{3,2,1,0:T(8,128)S(1)} %fusion.15, f32[3,16,2,128]{3,2,1,0:T(2,128)S(1)} %collective-permute-done.10, f32[16,64,128]{2,1,0:T(8,128)S(1)} %get-tuple-element.42, f32[16,64,128]{2,1,0:T(8,128)S(1)} %get-tuple-element.43, ...), kind=kLoop, calls=%fused_computation.47 | loop fusion | flops 5111808 | bytes 5865472 | tf_op jit(solution)/shard_map/add | solution.py:73
  (70 shorter events, 0.7 us)
Async XLA Ops:
  0.6 16.8 %copy-start.16 = (s32[1152]{0:T(1024)S(1)}, s32[1152]{0:T(1024)}, u32[]{:S(2)}) copy-start(s32[1152]{0:T(1024)} %param.10) | copy-start | bytes 13828
  0.6 23.3 %copy-start.12 = (s32[3,1152]{1,0:T(4,128)S(1)}, s32[3,1152]{1,0:T(4,128)}, u32[]{:S(2)}) copy-start(s32[3,1152]{1,0:T(4,128)} %param.11) | copy-start | bytes 41476
  2.5 22.8 %copy-start.13 = (f32[3,1152]{1,0:T(4,128)S(1)}, f32[3,1152]{1,0:T(4,128)}, u32[]{:S(2)}) copy-start(f32[3,1152]{1,0:T(4,128)} %param.12) | copy-start | bytes 41476
  2.5 87.8 %collective-permute-start = (f32[3,2,64,128]{3,2,1,0:T(8,128)}, f32[3,2,64,128]{3,2,1,0:T(8,128)}, u32[]{:S(2)}, u32[]{:S(2)}) collective-permute-start(f32[3,2,64,128]{3,2,1,0:T(8,128)} %get-tuple-element.33), channel_id=1, source_target_pairs={{0,2},{2,4},{4,6},{6,8},{8,10},{10,12},{12,14},{14,16},{16,18},{18... | collective-permute-start | bytes 589832 | tf_op jit(solution)/shard_map/ppermute | solution.py:22
  4.5 87.3 %collective-permute-start.1 = (f32[3,2,64,128]{3,2,1,0:T(8,128)}, f32[3,2,64,128]{3,2,1,0:T(8,128)}, u32[]{:S(2)}, u32[]{:S(2)}) collective-permute-start(f32[3,2,64,128]{3,2,1,0:T(8,128)} %get-tuple-element.32), channel_id=1, source_target_pairs={{2,0},{4,2},{6,4},{8,6},{10,8},{12,10},{14,12},{16,14},{18,16},{20... | collective-permute-start | bytes 589832 | tf_op jit(solution)/shard_map/ppermute | solution.py:23
  10.8 16.2 %copy-start = (f32[3,16,64,128]{3,2,1,0:T(8,128)S(1)}, f32[3,16,64,128]{3,2,1,0:T(8,128)}, u32[]{:S(2)}) copy-start(f32[3,16,64,128]{3,2,1,0:T(8,128)} %param.9) | copy-start | bytes 4718596
  10.8 88.3 %collective-permute-start.4 = (f32[3,2,64,128]{3,2,1,0:T(8,128)}, f32[3,2,64,128]{3,2,1,0:T(8,128)}, u32[]{:S(2)}, u32[]{:S(2)}) collective-permute-start(f32[3,2,64,128]{3,2,1,0:T(8,128)} %get-tuple-element.35), channel_id=1, source_target_pairs={{0,2},{2,4},{4,6},{6,8},{8,10},{10,12},{12,14},{14,16},{16,18},{18... | collective-permute-start | bytes 589832 | tf_op jit(solution)/shard_map/ppermute | solution.py:22
  12.8 87.8 %collective-permute-start.5 = (f32[3,2,64,128]{3,2,1,0:T(8,128)S(1)}, f32[3,2,64,128]{3,2,1,0:T(8,128)}, u32[]{:S(2)}, u32[]{:S(2)}) collective-permute-start(f32[3,2,64,128]{3,2,1,0:T(8,128)S(1)} %get-tuple-element.34), channel_id=1, source_target_pairs={{2,0},{4,2},{6,4},{8,6},{10,8},{12,10},{14,12},{16,14},{18,16},{20... | collective-permute-start | bytes 589832 | tf_op jit(solution)/shard_map/ppermute | solution.py:23
  25.2 1.3 copy-start.17
  26.5 0.6 copy-start.19
  33.4 44.9 %copy-start.14 = (f32[1152]{0:T(1024)S(1)}, f32[1152]{0:T(1024)}, u32[]{:S(2)}) copy-start(f32[1152]{0:T(1024)} %param.14) | copy-start | bytes 13828
  33.4 44.9 %copy-start.15 = (f32[1152]{0:T(1024)S(1)}, f32[1152]{0:T(1024)}, u32[]{:S(2)}) copy-start(f32[1152]{0:T(1024)} %param.13) | copy-start | bytes 13828
  33.4 45.3 %copy-start.2 = (f32[3,16,64,128]{3,2,1,0:T(8,128)S(1)}, f32[3,16,64,128]{3,2,1,0:T(8,128)}, u32[]{:S(2)}) copy-start(f32[3,16,64,128]{3,2,1,0:T(8,128)} %param.8) | copy-start | bytes 4718596
  78.7 2.0 %copy-start.1 = (f32[3,16,64,128]{3,2,1,0:T(8,128)S(1)}, f32[3,16,64,128]{3,2,1,0:T(8,128)}, u32[]{:S(2)}) copy-start(f32[3,16,64,128]{3,2,1,0:T(8,128)} %param.9) | copy-start | bytes 4718596
  82.4 7.2 %copy-start.8 = (f32[3,1152]{1,0:T(4,128)}, f32[3,1152]{1,0:T(4,128)S(1)}, u32[]{:S(2)}) copy-start(f32[3,1152]{1,0:T(4,128)S(1)} %pad_maximum_fusion.9) | copy-start | bytes 41476
  91.8 7.3 %copy-start.10 = (f32[3,18,64,128]{3,2,1,0:T(8,128)}, f32[3,18,64,128]{3,2,1,0:T(8,128)S(1)}, u32[]{:S(2)}) copy-start(f32[3,18,64,128]{3,2,1,0:T(8,128)S(1)} %get-tuple-element.26) | copy-start | bytes 5308420
  93.0 6.1 %copy-start.6 = (f32[3,18,64,128]{3,2,1,0:T(8,128)}, f32[3,18,64,128]{3,2,1,0:T(8,128)S(1)}, u32[]{:S(2)}) copy-start(f32[3,18,64,128]{3,2,1,0:T(8,128)S(1)} %get-tuple-element.52) | copy-start | bytes 5308420
  93.0 16.6 %copy-start.3 = (f32[3,20,64,128]{3,2,1,0:T(8,128)}, f32[3,20,64,128]{3,2,1,0:T(8,128)S(1)}, u32[]{:S(2)}) copy-start(f32[3,20,64,128]{3,2,1,0:T(8,128)S(1)} %get-tuple-element.53) | copy-start | bytes 5898244
  93.1 14.8 %collective-permute-start.2 = (f32[3,20,2,128]{3,2,1,0:T(2,128)S(1)}, f32[3,20,2,128]{3,2,1,0:T(2,128)S(1)}, u32[]{:S(2)}, u32[]{:S(2)}) collective-permute-start(f32[3,20,2,128]{3,2,1,0:T(2,128)S(1)} %get-tuple-element.13), channel_id=1, source_target_pairs={{0,1},{2,3},{4,5},{6,7},{8,9},{10,11},{12,13},{14,15},{16,17},{18,... | collective-permute-start | bytes 184328 | tf_op jit(solution)/shard_map/ppermute | solution.py:22
  94.4 13.5 %collective-permute-start.3 = (f32[3,20,2,128]{3,2,1,0:T(2,128)S(1)}, f32[3,20,2,128]{3,2,1,0:T(2,128)S(1)}, u32[]{:S(2)}, u32[]{:S(2)}) collective-permute-start(f32[3,20,2,128]{3,2,1,0:T(2,128)S(1)} %get-tuple-element.14), channel_id=1, source_target_pairs={{1,0},{3,2},{5,4},{7,6},{9,8},{11,10},{13,12},{15,14},{17,16},{19,... | collective-permute-start | bytes 184328 | tf_op jit(solution)/shard_map/ppermute | solution.py:23
  100.7 13.7 %copy-start.11 = (f32[3,18,64,128]{3,2,1,0:T(8,128)}, f32[3,18,64,128]{3,2,1,0:T(8,128)S(1)}, u32[]{:S(2)}) copy-start(f32[3,18,64,128]{3,2,1,0:T(8,128)S(1)} %get-tuple-element.29) | copy-start | bytes 5308420
  101.9 7.7 %copy-start.7 = (f32[3,18,64,128]{3,2,1,0:T(8,128)}, f32[3,18,64,128]{3,2,1,0:T(8,128)S(1)}, u32[]{:S(2)}) copy-start(f32[3,18,64,128]{3,2,1,0:T(8,128)S(1)} %get-tuple-element.56) | copy-start | bytes 5308420
  101.9 8.9 %copy-start.4 = (f32[3,20,64,128]{3,2,1,0:T(8,128)}, f32[3,20,64,128]{3,2,1,0:T(8,128)S(1)}, u32[]{:S(2)}) copy-start(f32[3,20,64,128]{3,2,1,0:T(8,128)S(1)} %get-tuple-element.57) | copy-start | bytes 5898244
  102.0 8.8 %collective-permute-start.6 = (f32[3,20,2,128]{3,2,1,0:T(2,128)S(1)}, f32[3,20,2,128]{3,2,1,0:T(2,128)S(1)}, u32[]{:S(2)}, u32[]{:S(2)}) collective-permute-start(f32[3,20,2,128]{3,2,1,0:T(2,128)S(1)} %get-tuple-element.15), channel_id=1, source_target_pairs={{0,1},{2,3},{4,5},{6,7},{8,9},{10,11},{12,13},{14,15},{16,17},{18,... | collective-permute-start | bytes 184328 | tf_op jit(solution)/shard_map/ppermute | solution.py:22
  103.3 7.5 %collective-permute-start.7 = (f32[3,20,2,128]{3,2,1,0:T(2,128)S(1)}, f32[3,20,2,128]{3,2,1,0:T(2,128)S(1)}, u32[]{:S(2)}, u32[]{:S(2)}) collective-permute-start(f32[3,20,2,128]{3,2,1,0:T(2,128)S(1)} %get-tuple-element.16), channel_id=1, source_target_pairs={{1,0},{3,2},{5,4},{7,6},{9,8},{11,10},{13,12},{15,14},{17,16},{19,... | collective-permute-start | bytes 184328 | tf_op jit(solution)/shard_map/ppermute | solution.py:23
  110.8 3.6 %copy-start.9 = (f32[192,16,3]{0,1,2:T(8,128)S(1)}, f32[192,16,3]{0,1,2:T(8,128)}, u32[]{:S(2)}) copy-start(f32[192,16,3]{0,1,2:T(8,128)} %broadcast_multiply_fusion) | copy-start | bytes 110596
  110.8 3.6 %copy-start.18 = (s32[192]{0:T(256)S(1)}, s32[192]{0:T(256)}, u32[]{:S(2)}) copy-start(s32[192]{0:T(256)} %copy-done.17) | copy-start | bytes 2308
  110.8 3.6 %copy-start.20 = (f32[192]{0:T(256)S(1)}, f32[192]{0:T(256)}, u32[]{:S(2)}) copy-start(f32[192]{0:T(256)} %copy-done.19) | copy-start | bytes 2308
  114.4 20.4 %copy-start.5 = (f32[16,64,128]{2,1,0:T(8,128)S(1)}, f32[16,64,128]{2,1,0:T(8,128)}, u32[]{:S(2)}) copy-start(f32[16,64,128]{2,1,0:T(8,128)} %get-tuple-element.21) | copy-start | bytes 1572868
  141.2 7.1 %collective-permute-start.8 = (f32[3,2,64,128]{3,2,1,0:T(8,128)S(1)}, f32[3,2,64,128]{3,2,1,0:T(8,128)S(1)}, u32[]{:S(2)}, u32[]{:S(2)}) collective-permute-start(f32[3,2,64,128]{3,2,1,0:T(8,128)S(1)} %get-tuple-element.19), channel_id=1, source_target_pairs={{2,0},{4,2},{6,4},{8,6},{10,8},{12,10},{14,12},{16,14},{18,16},{20... | collective-permute-start | bytes 589832 | tf_op jit(solution)/shard_map/ppermute | solution.py:23
  143.1 7.9 %collective-permute-start.9 = (f32[3,2,64,128]{3,2,1,0:T(8,128)S(1)}, f32[3,2,64,128]{3,2,1,0:T(8,128)S(1)}, u32[]{:S(2)}, u32[]{:S(2)}) collective-permute-start(f32[3,2,64,128]{3,2,1,0:T(8,128)S(1)} %get-tuple-element.20), channel_id=1, source_target_pairs={{0,2},{2,4},{4,6},{6,8},{8,10},{10,12},{12,14},{14,16},{16,18},{18... | collective-permute-start | bytes 589832 | tf_op jit(solution)/shard_map/ppermute | solution.py:22
  152.4 6.1 %collective-permute-start.10 = (f32[3,16,2,128]{3,2,1,0:T(2,128)S(1)}, f32[3,16,2,128]{3,2,1,0:T(2,128)S(1)}, u32[]{:S(2)}, u32[]{:S(2)}) collective-permute-start(f32[3,16,2,128]{3,2,1,0:T(2,128)S(1)} %get-tuple-element.17), channel_id=1, source_target_pairs={{1,0},{3,2},{5,4},{7,6},{9,8},{11,10},{13,12},{15,14},{17,16},{19,... | collective-permute-start | bytes 147464 | tf_op jit(solution)/shard_map/ppermute | solution.py:23
  155.5 6.0 %collective-permute-start.11 = (f32[3,16,2,128]{3,2,1,0:T(2,128)S(1)}, f32[3,16,2,128]{3,2,1,0:T(2,128)S(1)}, u32[]{:S(2)}, u32[]{:S(2)}) collective-permute-start(f32[3,16,2,128]{3,2,1,0:T(2,128)S(1)} %get-tuple-element.18), channel_id=1, source_target_pairs={{0,1},{2,3},{4,5},{6,7},{8,9},{10,11},{12,13},{14,15},{16,17},{18,... | collective-permute-start | bytes 147464 | tf_op jit(solution)/shard_map/ppermute | solution.py:22
where the time goes:
time: 164 us
  blocking collectives  40.4 us (25%)
  starting transfers between devices  33.8 us (21%)
  other arithmetic  33.1 us (20%)
  matrix products  25.8 us (16%)
  local copies, waits for them, and re-layouts  22.7 us (14%)
  waiting for transfers between devices  5.74 us (4%)
  between operations  1.99 us (1%)
    psum x1, blocking collectives, on_device(): point_velocity = lax.psum(partial_velocity, ('gy', 'gz'))  40.4 us
    ppermute x6, starting transfers between devices, with_halo(): after = lax.ppermute(initial, axis, down)  23.4 us
    dot_general x1, matrix products, on_device(): jnp.dot(spread.reshape(-1, spread.shape[3]), table_x.T, precision=highest...  20.4 us
    ppermute x6, starting transfers between devices, with_halo(): before = lax.ppermute(last, axis, up)  10.4 us
    add x3, other arithmetic, remesh_padded(): total = total + remesh_kernel(offset - moved)[None] * part  9.8 us
    select_n x4, other arithmetic, remesh_kernel(): return jnp.where(mag < 1.0, inner, jnp.where(mag < 2.0, outer, 0.0))  7.58 us
    unnamed x47, local copies, waits for them, and re-layouts  6.02 us
    ppermute x6, waiting for transfers between devices, with_halo(): before = lax.ppermute(last, axis, up)  5.72 us
  transfers between devices with their start and end apart: 12, of which 2 were waited for; matrix products, arithmetic and copies ran while one was open for 27% of the time, Pallas kernels for 0%

commit v1 on v0

--- a/solution.py
+++ b/solution.py
@@ -2,6 +2,7 @@
 import jax.numpy as jnp
 from jax import lax
 from jax.sharding import PartitionSpec as P
+from jax.lax import all_gather
 
 TURBINES = 6
 BLADES = 3
@@ -173,7 +174,7 @@
     partial_velocity = jnp.dot(
         compact, selector, precision=highest, preferred_element_type=jnp.float32
     )
-    point_velocity = lax.psum(partial_velocity, ("gy", "gz"))
+    point_velocity = jnp.sum(all_gather(partial_velocity, ("gy", "gz")), axis=0)
     sources = blade_forces(point_velocity, chord, twist, angle_step)
     local_sources = sources[:, picked]
     spread = jnp.einsum("cq,yq,zq->cyzq", local_sources, table_y, table_z, precision=highest)

time: 164 us -> 189 us (1.15)
  the two profiles are of different devices: /device:TPU:10 before, /device:TPU:6 now
where the time goes in v1:
time: 189 us; the launch traced here: 188 us
  blocking collectives  59.8 us (32%)
  starting transfers between devices  36.9 us (20%)
  other arithmetic  33.3 us (18%)
  matrix products  25.8 us (14%)
  local copies, waits for them, and re-layouts  22.7 us (12%)
  waiting for transfers between devices  7.84 us (4%)
  between operations  1.99 us (1%)
    all_gather x1, blocking collectives, on_device(): point_velocity = jnp.sum(all_gather(partial_velocity, ('gy', 'gz')), axis=0)  59.8 us
    ppermute x6, starting transfers between devices, with_halo(): after = lax.ppermute(initial, axis, down)  27 us
    dot_general x1, matrix products, on_device(): jnp.dot(spread.reshape(-1, spread.shape[3]), table_x.T, precision=highest...  20.4 us
    ppermute x6, starting transfers between devices, with_halo(): before = lax.ppermute(last, axis, up)  9.88 us
    add x3, other arithmetic, remesh_padded(): total = total + remesh_kernel(offset - moved)[None] * part  9.8 us
    ppermute x6, waiting for transfers between devices, with_halo(): before = lax.ppermute(last, axis, up)  7.83 us
    select_n x4, other arithmetic, remesh_kernel(): return jnp.where(mag < 1.0, inner, jnp.where(mag < 2.0, outer, 0.0))  7.58 us
    unnamed x47, local copies, waits for them, and re-layouts  6.02 us
  transfers between devices with their start and end apart: 12, of which 2 were waited for; matrix products, arithmetic and copies ran while one was open for 24% of the time, Pallas kernels for 0%

profile of v1, /device:TPU:6, one launch (start us, length us, event | category | flops | bytes accessed | tf_op | source)
XLA Modules:
  0.0 188.3 jit_solution(11001651823822679618)
XLA Ops:
  0.6 1.8 fusion.251
  2.5 2.0 %collective-permute-start = (f32[3,2,64,128]{3,2,1,0:T(8,128)}, f32[3,2,64,128]{3,2,1,0:T(8,128)}, u32[]{:S(2)}, u32[]{:S(2)}) collective-permute-start(f32[3,2,64,128]{3,2,1,0:T(8,128)} %get-tuple-element.37), channel_id=1, source_target_pairs={{0,2},{2,4},{4,6},{6,8},{8,10},{10,12},{12,14},{14,16},{16,18},{18... | collective-permute-start | bytes 589832 | tf_op jit(solution)/shard_map/ppermute | solution.py:23
  4.5 3.6 %collective-permute-start.1 = (f32[3,2,64,128]{3,2,1,0:T(8,128)}, f32[3,2,64,128]{3,2,1,0:T(8,128)}, u32[]{:S(2)}, u32[]{:S(2)}) collective-permute-start(f32[3,2,64,128]{3,2,1,0:T(8,128)} %get-tuple-element.36), channel_id=1, source_target_pairs={{2,0},{4,2},{6,4},{8,6},{10,8},{12,10},{14,12},{16,14},{18,16},{20... | collective-permute-start | bytes 589832 | tf_op jit(solution)/shard_map/ppermute | solution.py:24
  8.2 1.7 fusion.252
  9.9 2.0 %collective-permute-start.4 = (f32[3,2,64,128]{3,2,1,0:T(8,128)}, f32[3,2,64,128]{3,2,1,0:T(8,128)}, u32[]{:S(2)}, u32[]{:S(2)}) collective-permute-start(f32[3,2,64,128]{3,2,1,0:T(8,128)} %get-tuple-element.39), channel_id=1, source_target_pairs={{0,2},{2,4},{4,6},{6,8},{8,10},{10,12},{12,14},{14,16},{16,18},{18... | collective-permute-start | bytes 589832 | tf_op jit(solution)/shard_map/ppermute | solution.py:23
  11.9 3.6 %collective-permute-start.5 = (f32[3,2,64,128]{3,2,1,0:T(8,128)S(1)}, f32[3,2,64,128]{3,2,1,0:T(8,128)}, u32[]{:S(2)}, u32[]{:S(2)}) collective-permute-start(f32[3,2,64,128]{3,2,1,0:T(8,128)S(1)} %get-tuple-element.38), channel_id=1, source_target_pairs={{2,0},{4,2},{6,4},{8,6},{10,8},{12,10},{14,12},{16,14},{18,16},{20... | collective-permute-start | bytes 589832 | tf_op jit(solution)/shard_map/ppermute | solution.py:24
  15.6 5.0 %sort.17 = (s32[1152]{0:T(1024)}, s32[1152]{0:T(1024)S(1)}) sort(s32[1152]{0:T(1024)S(1)} %get-tuple-element.67, s32[1152]{0:T(1024)S(1)} %iota.43), dimensions={0}, to_apply=%region_0.1 | sort | flops 12672 | bytes 18432 | tf_op jit(solution)/shard_map/jit(argsort)/sort | solution.py:153
  20.7 1.4 gather_fusion.3
  22.2 0.2 copy.22
  22.4 0.7 gather_fusion.1
  23.1 0.3 slice_reduce_fusion.5
  23.4 0.2 copy.23
  23.7 0.7 gather_fusion.2
  24.4 0.3 slice_reduce_fusion.4
  24.7 0.5 copy-done.19
  25.2 3.6 %convolution_bitcast_fusion = f32[3072,192]{0,1:T(8,128)} fusion(f32[3072,128]{1,0:T(8,128)S(1)} %bitcast.51, f32[192]{0:T(256)S(1)} %get-tuple-element.12, s32[192]{0:T(256)S(1)} %get-tuple-element.9), kind=kOutput, calls=%fused_computation.18 | convolution fusion | flops 906461184 | bytes 3933696 | tf_op jit(solution)/shard_map/dot_general | solution.py:166
  28.8 2.2 %copy.37 = f32[3072,192]{1,0:T(8,128)S(1)} copy(f32[3072,192]{0,1:T(8,128)} %convolution_bitcast_fusion) | data formatting | bytes 4718592
  31.0 0.1 fusion.187
  31.2 0.4 multiply_reduce_fusion
  31.6 0.2 copy.33
  31.9 1.4 gather_fusion
  33.3 0.1 fusion.222
  33.4 0.1 copy.34
  33.5 1.4 fusion.254
  34.9 0.5 convolution_bitcast_fusion.1
  35.4 59.8 %all-gather.1 = f32[32,3,1152]{2,1,0:T(4,128)S(1)} all-gather(f32[1,3,1152]{2,1,0:T(4,128)S(1)} %convolution_bitcast_fusion.1), channel_id=2, replica_groups=mesh['gy'=16,'gz'=2] {'gy','gz'}, dimensions={0}, use_global_device_ids=true | all-gather | bytes 456192 | tf_op jit(solution)/shard_map/all_gather | solution.py:177
  95.2 0.1 reduce_sum.9
  96.1 0.1 add_multiply_fusion
  96.5 1.2 multiply_bitcast_fusion.2
  97.7 0.8 copy-done.1
  98.4 1.3 fusion.103
  99.8 0.2 rsqrt_multiply_fusion
  100.0 0.1 divide_add_fusion.1
  100.1 1.1 copy.25
  101.2 1.7 gather_fusion.4
  103.0 4.3 %fusion.92 = (f32[16,64,128]{2,1,0:T(8,128)}, f32[16,64,128]{2,1,0:T(8,128)}, f32[16,64,128]{2,1,0:T(8,128)}, f32[16,64,128]{2,1,0:T(8,128)}) fusion(f32[16,64,128]{2,1,0:T(8,128)} %get-tuple-element.26), kind=kLoop, calls=%fused_computation.199 | loop fusion | flops 9437184 | bytes 2621440 | tf_op jit(solution)/shard_map/jit(_where)/select_n | solution.py:33
  107.3 0.6 broadcast_multiply_fusion
  108.0 1.0 constant_dynamic-update-slice_fusion.4
  108.9 0.6 constant_dynamic-update-slice_fusion.3
  109.5 1.2 constant_dynamic-update-slice_fusion.5
  110.8 1.3 collective-permute-start.2
  112.1 6.5 %collective-permute-start.3 = (f32[3,20,2,128]{3,2,1,0:T(2,128)S(1)}, f32[3,20,2,128]{3,2,1,0:T(2,128)S(1)}, u32[]{:S(2)}, u32[]{:S(2)}) collective-permute-start(f32[3,20,2,128]{3,2,1,0:T(2,128)S(1)} %get-tuple-element.18), channel_id=1, source_target_pairs={{1,0},{3,2},{5,4},{7,6},{9,8},{11,10},{13,12},{15,14},{17,16},{19,... | collective-permute-start | bytes 184328 | tf_op jit(solution)/shard_map/ppermute | solution.py:24
  118.6 1.0 constant_dynamic-update-slice_fusion.8
  119.6 0.6 constant_dynamic-update-slice_fusion.7
  120.2 1.2 constant_dynamic-update-slice_fusion.9
  121.5 1.3 collective-permute-start.6
  122.8 4.7 %collective-permute-start.7 = (f32[3,20,2,128]{3,2,1,0:T(2,128)S(1)}, f32[3,20,2,128]{3,2,1,0:T(2,128)S(1)}, u32[]{:S(2)}, u32[]{:S(2)}) collective-permute-start(f32[3,20,2,128]{3,2,1,0:T(2,128)S(1)} %get-tuple-element.20), channel_id=1, source_target_pairs={{1,0},{3,2},{5,4},{7,6},{9,8},{11,10},{13,12},{15,14},{17,16},{19,... | collective-permute-start | bytes 184328 | tf_op jit(solution)/shard_map/ppermute | solution.py:24
  127.5 1.7 pad_maximum_fusion
  129.3 1.2 slice_bitcast_fusion
  130.5 3.5 %select_maximum_fusion = f32[3,20,68,132]{3,2,1,0:T(8,128)} fusion(f32[3,20,2,128]{3,2,1,0:T(2,128)S(1)} %collective-permute-done.7, f32[3,20,64,128]{3,2,1,0:T(8,128)S(1)} %get-tuple-element.61, f32[3,20,2,128]{3,2,1,0:T(2,128)S(1)} %collective-permute-done.6), kind=kLoop, calls=%fused_computation.15 | loop fusion | flops 4308480 | bytes 4243200 | tf_op jit(solution)/shard_map/concatenate | solution.py:25
  134.1 20.4 %fusion.30 = f32[3,16,64,128]{3,2,1,0:T(8,128)} fusion(f32[3,16,64,128]{3,2,1,0:T(8,128)S(1)} %copy-done.2, f32[3,20,64,128]{3,2,1,0:T(8,128)} %copy-done.4, f32[3,20,2,128]{3,2,1,0:T(2,128)S(1)} %collective-permute-done.7, f32[3,20,2,128]{3,2,1,0:T(2,128)S(1)} %collective-permute-done.6, f32[3,20,64,128]{3,2,1,0:T(8,128)} %copy-done.3, ...), kind=kOutput, calls=%fused_computation.71 | convolution fusion | flops 929464320 | bytes 29947392 | tf_op jit(solution)/shard_map/dot_general | solution.py:181
  154.4 6.4 %fusion.48 = f32[3,16,64,128]{3,2,1,0:T(8,128)S(1)} fusion(f32[3,16,64,128]{3,2,1,0:T(8,128)} %fusion.30, f32[16,64,128]{2,1,0:T(8,128)} %get-tuple-element.53, f32[16,64,128]{2,1,0:T(8,128)} %get-tuple-element.52, f32[16,64,128]{2,1,0:T(8,128)S(1)} %copy-done.5, f32[16,64,128]{2,1,0:T(8,128)} %get-tuple-element.51, f32[16,64,128]{2,1,0:T(8,128)} %get-tuple-element.50), kind=kLoop, calls=%fused_computation.89 | loop fusion | flops 3538944 | bytes 5767168 | tf_op jit(solution)/shard_map/add | solution.py:74
  160.9 5.6 %collective-permute-start.8 = (f32[3,2,64,128]{3,2,1,0:T(8,128)S(1)}, f32[3,2,64,128]{3,2,1,0:T(8,128)S(1)}, u32[]{:S(2)}, u32[]{:S(2)}) collective-permute-start(f32[3,2,64,128]{3,2,1,0:T(8,128)S(1)} %get-tuple-element.23), channel_id=1, source_target_pairs={{2,0},{4,2},{6,4},{8,6},{10,8},{12,10},{14,12},{16,14},{18,16},{20... | collective-permute-start | bytes 589832 | tf_op jit(solution)/shard_map/ppermute | solution.py:24
  166.5 1.9 %collective-permute-start.9 = (f32[3,2,64,128]{3,2,1,0:T(8,128)S(1)}, f32[3,2,64,128]{3,2,1,0:T(8,128)S(1)}, u32[]{:S(2)}, u32[]{:S(2)}) collective-permute-start(f32[3,2,64,128]{3,2,1,0:T(8,128)S(1)} %get-tuple-element.24), channel_id=1, source_target_pairs={{0,2},{2,4},{4,6},{6,8},{8,10},{10,12},{12,14},{14,16},{16,18},{18... | collective-permute-start | bytes 589832 | tf_op jit(solution)/shard_map/ppermute | solution.py:23
  168.4 0.1 fusion.77
  168.5 1.5 fusion.87
  170.0 1.1 fusion.79
  171.2 4.8 %collective-permute-done.9 = f32[3,2,64,128]{3,2,1,0:T(8,128)S(1)} collective-permute-done((f32[3,2,64,128]{3,2,1,0:T(8,128)S(1)}, f32[3,2,64,128]{3,2,1,0:T(8,128)S(1)}, u32[]{:S(2)}, u32[]{:S(2)}) %collective-permute-start.9) | collective-permute-done | bytes 196640 | tf_op jit(solution)/shard_map/ppermute | solution.py:23
  176.0 1.3 fusion.15
  177.3 2.9 %collective-permute-start.10 = (f32[3,16,2,128]{3,2,1,0:T(2,128)S(1)}, f32[3,16,2,128]{3,2,1,0:T(2,128)S(1)}, u32[]{:S(2)}, u32[]{:S(2)}) collective-permute-start(f32[3,16,2,128]{3,2,1,0:T(2,128)S(1)} %get-tuple-element.21), channel_id=1, source_target_pairs={{1,0},{3,2},{5,4},{7,6},{9,8},{11,10},{13,12},{15,14},{17,16},{19,... | collective-permute-start | bytes 147464 | tf_op jit(solution)/shard_map/ppermute | solution.py:24
  180.3 1.3 collective-permute-start.11
  181.6 1.7 fusion.82
  183.2 3.0 %collective-permute-done.11 = f32[3,16,2,128]{3,2,1,0:T(2,128)S(1)} collective-permute-done((f32[3,16,2,128]{3,2,1,0:T(2,128)S(1)}, f32[3,16,2,128]{3,2,1,0:T(2,128)S(1)}, u32[]{:S(2)}, u32[]{:S(2)}) %collective-permute-start.11) | collective-permute-done | bytes 49184 | tf_op jit(solution)/shard_map/ppermute | solution.py:23
  186.3 2.1 %fusion.7 = f32[3,16,64,128]{3,2,1,0:T(8,128)} fusion(f32[3,16,2,128]{3,2,1,0:T(2,128)S(1)} %collective-permute-done.11, f32[3,16,64,128]{3,2,1,0:T(8,128)S(1)} %fusion.15, f32[3,16,2,128]{3,2,1,0:T(2,128)S(1)} %collective-permute-done.10, f32[16,64,128]{2,1,0:T(8,128)S(1)} %get-tuple-element.46, f32[16,64,128]{2,1,0:T(8,128)S(1)} %get-tuple-element.47, ...), kind=kLoop, calls=%fused_computation.48 | loop fusion | flops 5111808 | bytes 5865472 | tf_op jit(solution)/shard_map/add | solution.py:74
  (71 shorter events, 0.8 us)
Async XLA Ops:
  0.6 15.0 %copy-start.16 = (s32[1152]{0:T(1024)S(1)}, s32[1152]{0:T(1024)}, u32[]{:S(2)}) copy-start(s32[1152]{0:T(1024)} %param.10) | copy-start | bytes 13828
  0.6 21.5 %copy-start.12 = (s32[3,1152]{1,0:T(4,128)S(1)}, s32[3,1152]{1,0:T(4,128)}, u32[]{:S(2)}) copy-start(s32[3,1152]{1,0:T(4,128)} %param.11) | copy-start | bytes 41476
  2.5 21.0 %copy-start.13 = (f32[3,1152]{1,0:T(4,128)S(1)}, f32[3,1152]{1,0:T(4,128)}, u32[]{:S(2)}) copy-start(f32[3,1152]{1,0:T(4,128)} %param.12) | copy-start | bytes 41476
  2.5 105.5 %collective-permute-start = (f32[3,2,64,128]{3,2,1,0:T(8,128)}, f32[3,2,64,128]{3,2,1,0:T(8,128)}, u32[]{:S(2)}, u32[]{:S(2)}) collective-permute-start(f32[3,2,64,128]{3,2,1,0:T(8,128)} %get-tuple-element.37), channel_id=1, source_target_pairs={{0,2},{2,4},{4,6},{6,8},{8,10},{10,12},{12,14},{14,16},{16,18},{18... | collective-permute-start | bytes 589832 | tf_op jit(solution)/shard_map/ppermute | solution.py:23
  4.5 105.0 %collective-permute-start.1 = (f32[3,2,64,128]{3,2,1,0:T(8,128)}, f32[3,2,64,128]{3,2,1,0:T(8,128)}, u32[]{:S(2)}, u32[]{:S(2)}) collective-permute-start(f32[3,2,64,128]{3,2,1,0:T(8,128)} %get-tuple-element.36), channel_id=1, source_target_pairs={{2,0},{4,2},{6,4},{8,6},{10,8},{12,10},{14,12},{16,14},{18,16},{20... | collective-permute-start | bytes 589832 | tf_op jit(solution)/shard_map/ppermute | solution.py:24
  9.9 15.3 %copy-start = (f32[3,16,64,128]{3,2,1,0:T(8,128)S(1)}, f32[3,16,64,128]{3,2,1,0:T(8,128)}, u32[]{:S(2)}) copy-start(f32[3,16,64,128]{3,2,1,0:T(8,128)} %param.9) | copy-start | bytes 4718596
  9.9 108.7 %collective-permute-start.4 = (f32[3,2,64,128]{3,2,1,0:T(8,128)}, f32[3,2,64,128]{3,2,1,0:T(8,128)}, u32[]{:S(2)}, u32[]{:S(2)}) collective-permute-start(f32[3,2,64,128]{3,2,1,0:T(8,128)} %get-tuple-element.39), channel_id=1, source_target_pairs={{0,2},{2,4},{4,6},{6,8},{8,10},{10,12},{12,14},{14,16},{16,18},{18... | collective-permute-start | bytes 589832 | tf_op jit(solution)/shard_map/ppermute | solution.py:23
  11.9 108.3 %collective-permute-start.5 = (f32[3,2,64,128]{3,2,1,0:T(8,128)S(1)}, f32[3,2,64,128]{3,2,1,0:T(8,128)}, u32[]{:S(2)}, u32[]{:S(2)}) collective-permute-start(f32[3,2,64,128]{3,2,1,0:T(8,128)S(1)} %get-tuple-element.38), channel_id=1, source_target_pairs={{2,0},{4,2},{6,4},{8,6},{10,8},{12,10},{14,12},{16,14},{18,16},{20... | collective-permute-start | bytes 589832 | tf_op jit(solution)/shard_map/ppermute | solution.py:24
  23.4 1.3 copy-start.17
  24.7 0.6 copy-start.19
  31.8 64.2 %copy-start.14 = (f32[1152]{0:T(1024)S(1)}, f32[1152]{0:T(1024)}, u32[]{:S(2)}) copy-start(f32[1152]{0:T(1024)} %param.14) | copy-start | bytes 13828
  31.8 64.2 %copy-start.15 = (f32[1152]{0:T(1024)S(1)}, f32[1152]{0:T(1024)}, u32[]{:S(2)}) copy-start(f32[1152]{0:T(1024)} %param.13) | copy-start | bytes 13828
  31.8 64.6 %copy-start.2 = (f32[3,16,64,128]{3,2,1,0:T(8,128)S(1)}, f32[3,16,64,128]{3,2,1,0:T(8,128)}, u32[]{:S(2)}) copy-start(f32[3,16,64,128]{3,2,1,0:T(8,128)} %param.8) | copy-start | bytes 4718596
  96.4 2.0 %copy-start.1 = (f32[3,16,64,128]{3,2,1,0:T(8,128)S(1)}, f32[3,16,64,128]{3,2,1,0:T(8,128)}, u32[]{:S(2)}) copy-start(f32[3,16,64,128]{3,2,1,0:T(8,128)} %param.9) | copy-start | bytes 4718596
  100.1 7.2 %copy-start.8 = (f32[3,1152]{1,0:T(4,128)}, f32[3,1152]{1,0:T(4,128)S(1)}, u32[]{:S(2)}) copy-start(f32[3,1152]{1,0:T(4,128)S(1)} %pad_maximum_fusion.9) | copy-start | bytes 41476
  109.5 9.1 %copy-start.10 = (f32[3,18,64,128]{3,2,1,0:T(8,128)}, f32[3,18,64,128]{3,2,1,0:T(8,128)S(1)}, u32[]{:S(2)}) copy-start(f32[3,18,64,128]{3,2,1,0:T(8,128)S(1)} %get-tuple-element.30) | copy-start | bytes 5308420
  110.7 7.9 %copy-start.6 = (f32[3,18,64,128]{3,2,1,0:T(8,128)}, f32[3,18,64,128]{3,2,1,0:T(8,128)S(1)}, u32[]{:S(2)}) copy-start(f32[3,18,64,128]{3,2,1,0:T(8,128)S(1)} %get-tuple-element.56) | copy-start | bytes 5308420
  110.7 18.6 %copy-start.3 = (f32[3,20,64,128]{3,2,1,0:T(8,128)}, f32[3,20,64,128]{3,2,1,0:T(8,128)S(1)}, u32[]{:S(2)}) copy-start(f32[3,20,64,128]{3,2,1,0:T(8,128)S(1)} %get-tuple-element.57) | copy-start | bytes 5898244
  110.8 16.7 %collective-permute-start.2 = (f32[3,20,2,128]{3,2,1,0:T(2,128)S(1)}, f32[3,20,2,128]{3,2,1,0:T(2,128)S(1)}, u32[]{:S(2)}, u32[]{:S(2)}) collective-permute-start(f32[3,20,2,128]{3,2,1,0:T(2,128)S(1)} %get-tuple-element.17), channel_id=1, source_target_pairs={{0,1},{2,3},{4,5},{6,7},{8,9},{10,11},{12,13},{14,15},{16,17},{18,... | collective-permute-start | bytes 184328 | tf_op jit(solution)/shard_map/ppermute | solution.py:23
  112.1 15.4 %collective-permute-start.3 = (f32[3,20,2,128]{3,2,1,0:T(2,128)S(1)}, f32[3,20,2,128]{3,2,1,0:T(2,128)S(1)}, u32[]{:S(2)}, u32[]{:S(2)}) collective-permute-start(f32[3,20,2,128]{3,2,1,0:T(2,128)S(1)} %get-tuple-element.18), channel_id=1, source_target_pairs={{1,0},{3,2},{5,4},{7,6},{9,8},{11,10},{13,12},{15,14},{17,16},{19,... | collective-permute-start | bytes 184328 | tf_op jit(solution)/shard_map/ppermute | solution.py:24
  120.2 13.9 %copy-start.11 = (f32[3,18,64,128]{3,2,1,0:T(8,128)}, f32[3,18,64,128]{3,2,1,0:T(8,128)S(1)}, u32[]{:S(2)}) copy-start(f32[3,18,64,128]{3,2,1,0:T(8,128)S(1)} %get-tuple-element.33) | copy-start | bytes 5308420
  121.4 7.9 %copy-start.7 = (f32[3,18,64,128]{3,2,1,0:T(8,128)}, f32[3,18,64,128]{3,2,1,0:T(8,128)S(1)}, u32[]{:S(2)}) copy-start(f32[3,18,64,128]{3,2,1,0:T(8,128)S(1)} %get-tuple-element.60) | copy-start | bytes 5308420
  121.4 9.1 %copy-start.4 = (f32[3,20,64,128]{3,2,1,0:T(8,128)}, f32[3,20,64,128]{3,2,1,0:T(8,128)S(1)}, u32[]{:S(2)}) copy-start(f32[3,20,64,128]{3,2,1,0:T(8,128)S(1)} %get-tuple-element.61) | copy-start | bytes 5898244
  121.5 9.0 %collective-permute-start.6 = (f32[3,20,2,128]{3,2,1,0:T(2,128)S(1)}, f32[3,20,2,128]{3,2,1,0:T(2,128)S(1)}, u32[]{:S(2)}, u32[]{:S(2)}) collective-permute-start(f32[3,20,2,128]{3,2,1,0:T(2,128)S(1)} %get-tuple-element.19), channel_id=1, source_target_pairs={{0,1},{2,3},{4,5},{6,7},{8,9},{10,11},{12,13},{14,15},{16,17},{18,... | collective-permute-start | bytes 184328 | tf_op jit(solution)/shard_map/ppermute | solution.py:23
  122.8 7.7 %collective-permute-start.7 = (f32[3,20,2,128]{3,2,1,0:T(2,128)S(1)}, f32[3,20,2,128]{3,2,1,0:T(2,128)S(1)}, u32[]{:S(2)}, u32[]{:S(2)}) collective-permute-start(f32[3,20,2,128]{3,2,1,0:T(2,128)S(1)} %get-tuple-element.20), channel_id=1, source_target_pairs={{1,0},{3,2},{5,4},{7,6},{9,8},{11,10},{13,12},{15,14},{17,16},{19,... | collective-permute-start | bytes 184328 | tf_op jit(solution)/shard_map/ppermute | solution.py:24
  130.5 3.6 %copy-start.9 = (f32[192,16,3]{0,1,2:T(8,128)S(1)}, f32[192,16,3]{0,1,2:T(8,128)}, u32[]{:S(2)}) copy-start(f32[192,16,3]{0,1,2:T(8,128)} %broadcast_multiply_fusion) | copy-start | bytes 110596
  130.5 3.6 %copy-start.18 = (s32[192]{0:T(256)S(1)}, s32[192]{0:T(256)}, u32[]{:S(2)}) copy-start(s32[192]{0:T(256)} %copy-done.17) | copy-start | bytes 2308
  130.5 3.6 %copy-start.20 = (f32[192]{0:T(256)S(1)}, f32[192]{0:T(256)}, u32[]{:S(2)}) copy-start(f32[192]{0:T(256)} %copy-done.19) | copy-start | bytes 2308
  134.1 20.4 %copy-start.5 = (f32[16,64,128]{2,1,0:T(8,128)S(1)}, f32[16,64,128]{2,1,0:T(8,128)}, u32[]{:S(2)}) copy-start(f32[16,64,128]{2,1,0:T(8,128)} %get-tuple-element.25) | copy-start | bytes 1572868
  160.9 10.3 %collective-permute-start.8 = (f32[3,2,64,128]{3,2,1,0:T(8,128)S(1)}, f32[3,2,64,128]{3,2,1,0:T(8,128)S(1)}, u32[]{:S(2)}, u32[]{:S(2)}) collective-permute-start(f32[3,2,64,128]{3,2,1,0:T(8,128)S(1)} %get-tuple-element.23), channel_id=1, source_target_pairs={{2,0},{4,2},{6,4},{8,6},{10,8},{12,10},{14,12},{16,14},{18,16},{20... | collective-permute-start | bytes 589832 | tf_op jit(solution)/shard_map/ppermute | solution.py:24
  166.5 9.5 %collective-permute-start.9 = (f32[3,2,64,128]{3,2,1,0:T(8,128)S(1)}, f32[3,2,64,128]{3,2,1,0:T(8,128)S(1)}, u32[]{:S(2)}, u32[]{:S(2)}) collective-permute-start(f32[3,2,64,128]{3,2,1,0:T(8,128)S(1)} %get-tuple-element.24), channel_id=1, source_target_pairs={{0,2},{2,4},{4,6},{6,8},{8,10},{10,12},{12,14},{14,16},{16,18},{18... | collective-permute-start | bytes 589832 | tf_op jit(solution)/shard_map/ppermute | solution.py:23
  177.3 5.9 %collective-permute-start.10 = (f32[3,16,2,128]{3,2,1,0:T(2,128)S(1)}, f32[3,16,2,128]{3,2,1,0:T(2,128)S(1)}, u32[]{:S(2)}, u32[]{:S(2)}) collective-permute-start(f32[3,16,2,128]{3,2,1,0:T(2,128)S(1)} %get-tuple-element.21), channel_id=1, source_target_pairs={{1,0},{3,2},{5,4},{7,6},{9,8},{11,10},{13,12},{15,14},{17,16},{19,... | collective-permute-start | bytes 147464 | tf_op jit(solution)/shard_map/ppermute | solution.py:24
  180.3 6.0 %collective-permute-start.11 = (f32[3,16,2,128]{3,2,1,0:T(2,128)S(1)}, f32[3,16,2,128]{3,2,1,0:T(2,128)S(1)}, u32[]{:S(2)}, u32[]{:S(2)}) collective-permute-start(f32[3,16,2,128]{3,2,1,0:T(2,128)S(1)} %get-tuple-element.22), channel_id=1, source_target_pairs={{0,1},{2,3},{4,5},{6,7},{8,9},{10,11},{12,13},{14,15},{16,17},{18,... | collective-permute-start | bytes 147464 | tf_op jit(solution)/shard_map/ppermute | solution.py:23
